TPU v7x, 256 devices: a whole 4x4x8 slice. The times are simulated.
256 devices in a mesh: expert: 8 (over x, core), ffn: 32 (over z, y).
Axes of the slice: x: 4, y: 4, z: 8, core: 2. Of those that a mesh axis runs over, the one named last changes fastest.
Arguments:
- tokens: bfloat16 [8, 128, 4096], P('expert', 'ffn'), may hold values from -6 to 6
- routes: int32 [8, 128, 2], P('expert'), may hold values from 0 to 7, all different within a row; in each aligned block of 128 rows (0 to 127, 128 to 255, ..., all dimensions but the last counted through in order) at most 48 rows name the same one
- router: bfloat16 [4096, 8], replicated, may hold values from -0.09375 to 0.09375
- w_gate: bfloat16 [8, 4096, 12288], P('expert', None, 'ffn'), may hold values from -0.09375 to 0.09375
- w_up: bfloat16 [8, 4096, 12288], P('expert', None, 'ffn'), may hold values from -0.09375 to 0.09375
- w_down: bfloat16 [8, 12288, 4096], P('expert', 'ffn'), may hold values from -0.109375 to 0.109375
- adapter: bfloat16 [8, 4096, 4096], P('expert', None, 'ffn'), may hold values from -0.09375 to 0.09375
- upstream: bfloat16 [8, 128, 4096], P('expert', None, 'ffn'), may hold values from -24 to 24
- bound: float32 [8], P('expert'), may hold values from 2048 to 16384
Outputs:
- adapted: bfloat16 [8, 128, 4096], P('expert', None, 'ffn')
- clipped: bfloat16 [8, 4096, 4096], P('expert', None, 'ffn')
Inputs may be any that keep to these rules, and one draw needn't show every extreme that they name: `routes`: each token names two different experts; for each client at most 48 of its tokens name any one expert, and in some clients some expert is named by exactly 48 tokens.
All inputs are finite; a program needn't handle non-finite values.
Results may differ from a plain program's by a relative error of at most 0.015.
Values may be sent and summed in bfloat16 or wider, within the bound.
A program may use at most 64 MiB of HBM per device.

v0:
```python
import jax
import jax.numpy as jnp
from jax import lax
from jax.sharding import Mesh
from jax.sharding import PartitionSpec as P

FFN = ("ffn_0", "ffn_1")


def gathered_by_axis(value, axes, dim):
    out = value
    for number in range(len(axes) - 1, -1, -1):
        out = lax.all_gather(out, axes[number], axis=dim, tiled=True)
    return out


def own_rows(terms, axes):
    running = terms.astype(jnp.bfloat16)
    for axis in axes:
        running = lax.psum_scatter(running, axis, scatter_dimension=0, tiled=True)
    return running.astype(jnp.float32)


def in_order(parts, dim):
    dims = list(parts.shape[1:])
    dims[dim] *= parts.shape[0]
    return jnp.moveaxis(parts, 0, dim).reshape(dims)


def from_everyone(value, axis):
    copies = jnp.broadcast_to(value, (lax.axis_size(axis), *value.shape))
    return lax.all_to_all(copies, axis, split_axis=0, concat_axis=0, tiled=True)


def gathered_copies(value, axis, dim):
    return in_order(from_everyone(value, axis), dim)


def of_everyone(value, axis):
    everything = from_everyone(value, axis)
    return jnp.sum(everything, axis=0)


def slot_table(routed, expert_count):
    named_hits = jnp.sum(
        (routed[:, :, None] == jnp.arange(expert_count, dtype=jnp.int32)[None, None, :]).astype(
            jnp.int32
        ),
        axis=1,
    )
    before = jnp.cumsum(named_hits, axis=0) - named_hits
    return jnp.take_along_axis(before, routed, axis=1)


def pack_rows(token_rows, routed, expert_count, capacity):
    token_count = token_rows.shape[0]
    slot_flat = routed * capacity + slot_table(routed, expert_count)
    owners = jnp.repeat(jnp.arange(token_count, dtype=jnp.int32), 2)
    source = (
        jnp.full((expert_count * capacity,), token_count, jnp.int32)
        .at[slot_flat.reshape(-1)]
        .set(owners)
    )
    padded = jnp.concatenate(
        [token_rows, jnp.zeros((1, token_rows.shape[1]), token_rows.dtype)], axis=0
    )
    return (padded[source].reshape(expert_count, capacity, token_rows.shape[1]), slot_flat)


def mix_weights(token_rows, routed, router):
    logits = jnp.dot(token_rows, router, preferred_element_type=jnp.float32)
    picked = jnp.take_along_axis(logits, routed, axis=1)
    weight_first = jax.nn.sigmoid(picked[:, 0] - picked[:, 1])
    return (weight_first, 1.0 - weight_first)


def per_device(tokens, routes, router, w_gate, w_up, w_down, adapter, upstream, bound):
    expert_count = lax.axis_size("expert")
    gathered = gathered_by_axis(tokens, FFN, 1)
    token_rows = gathered[0]
    token_count = token_rows.shape[0]
    model_width = token_rows.shape[1]
    capacity = 3 * token_count // expert_count
    routed = routes[0]
    outgoing, slot_flat = pack_rows(token_rows, routed, expert_count, capacity)
    col_count = adapter.shape[2]
    column = lax.axis_index(FFN) * col_count
    weight_first, weight_second = mix_weights(token_rows, routed, router)
    arrived = lax.all_to_all(outgoing, "expert", split_axis=0, concat_axis=0, tiled=True)
    flat_rows = arrived.reshape(-1, model_width)
    gate_out = jnp.dot(flat_rows, w_gate[0], preferred_element_type=jnp.float32)
    up_out = jnp.dot(flat_rows, w_up[0], preferred_element_type=jnp.float32)
    hidden = (jax.nn.silu(gate_out) * up_out).astype(jnp.bfloat16)
    senders = arrived.shape[0]
    slots_here = arrived.shape[1]
    down_cols = w_down[0]
    term = lax.dot_general(
        down_cols, hidden, (((0,), (1,)), ((), ())), preferred_element_type=jnp.float32
    ).astype(jnp.bfloat16)
    term = lax.optimization_barrier(term).astype(jnp.float32)
    share = own_rows(
        jnp.transpose(term.reshape(col_count * lax.axis_size(FFN), senders, slots_here), (0, 2, 1)),
        FFN,
    )
    returned = lax.all_to_all(share, "expert", split_axis=2, concat_axis=2, tiled=True)
    slot_major = jnp.transpose(returned, (0, 2, 1)).reshape(col_count, -1)
    picked = slot_major[:, slot_flat]
    mix_cols = weight_first[None, :] * picked[:, :, 0] + weight_second[None, :] * picked[:, :, 1]
    own_tokens = lax.dynamic_slice_in_dim(token_rows, column, col_count, 1)
    own_layer = (own_tokens.astype(jnp.float32) + jnp.transpose(mix_cols)).astype(jnp.bfloat16)
    layer_out = gathered_copies(own_layer, FFN, 1)
    own_cols = lax.dynamic_slice_in_dim(layer_out, column, col_count, 1)
    adapted = (
        own_cols.astype(jnp.float32)
        + jnp.dot(layer_out, adapter[0], preferred_element_type=jnp.float32)
    ).astype(jnp.bfloat16)
    grad_input = upstream[0]
    adapter_grad = lax.dot_general(
        layer_out, grad_input, (((0,), (0,)), ((), ())), preferred_element_type=jnp.float32
    )
    squared = of_everyone(jnp.sum(adapter_grad * adapter_grad), FFN)
    grad_norm = jnp.sqrt(squared)
    clip_limit = bound[0]
    factor = clip_limit / jnp.maximum(grad_norm, clip_limit)
    clipped = (adapter_grad * factor).astype(jnp.bfloat16)
    return (adapted[None], clipped[None])


def solution(mesh):
    split = Mesh(mesh.devices.reshape(mesh.shape["expert"], 8, 4), ("expert", "ffn_0", "ffn_1"))
    placed = (
        P("expert", FFN, None),
        P("expert", None, None),
        P(),
        P("expert", None, FFN),
        P("expert", None, FFN),
        P("expert", FFN, None),
        P("expert", None, FFN),
        P("expert", None, FFN),
        P("expert"),
    )
    return jax.shard_map(
        per_device,
        mesh=split,
        in_specs=placed,
        out_specs=(P("expert", None, FFN), P("expert", None, FFN)),
        check_vma=False,
    )
```

profile of v0, /device:TPU:2, one launch (start us, length us, event | category | flops | bytes accessed | tf_op | source)
XLA Modules:
  0.0 286.1 jit_solution(3763902621592552826)
XLA Ops:
  7.2 1.0 copy.48
  8.2 12.8 %all_gather.6 = bf16[1,16,4096]{2,0,1:T(2,128)(2,1)S(1)} all-gather(bf16[1,4,4096]{2,0,1:T(2,128)(2,1)S(1)} %copy.48), channel_id=1, replica_groups=mesh['expert'=8,'ffn_0'=8,'ffn_1'=4] {'ffn_1'}, dimensions={1}, use_global_device_ids=true | all-gather | bytes 163840 | tf_op jit(solution)/shard_map/all_gather | solution.py:13
  21.0 0.8 copy.49
  21.8 0.8 copy.50
  22.6 0.7 convert_reduce_fusion
  23.3 0.1 copy.53
  23.4 0.1 squeeze.39
  23.6 0.1 reshape.235
  23.7 0.2 reduce_window_sum.11
  23.9 0.1 reshape.251
  24.1 1.9 gather_fusion.3
  26.0 1.4 scatter_custom_fusion
  27.5 35.2 %all-gather.2.cloned.1.call-done = bf16[1,128,4096]{2,1,0:T(8,128)(2,1)} async-done(((bf16[1,16,4096]{2,1,0:T(8,128)(2,1)}), bf16[1,128,4096]{2,1,0:T(8,128)(2,1)}) %all-gather.2.cloned.1.call-update) | async-done | bytes 1048592 | tf_op jit(solution)/shard_map/all_gather | solution.py:13
  62.7 2.3 concatenate.3
  65.0 9.7 %gather_fusion = bf16[384,4096]{1,0:T(8,128)(2,1)} fusion(bf16[129,4096]{1,0:T(8,128)(2,1)} %concatenate.3, s32[1024]{0:T(1024)S(1)} %pad_clamp_fusion.1), kind=kCustom, calls=%fused_computation | custom fusion | bytes 6292992 | tf_op jit(solution)/shard_map/gather | solution.py:67
  74.7 42.4 %all_to_all.21 = bf16[8,48,4096]{2,1,0:T(8,128)(2,1)S(1)} all-to-all(bf16[8,48,4096]{2,1,0:T(8,128)(2,1)} %bitcast.118), channel_id=1, replica_groups=mesh['expert'=8,'ffn_0'=8,'ffn_1'=4] {'expert'}, dimensions={0} | all-to-all | bytes 6291456 | tf_op jit(solution)/shard_map/all_to_all | solution.py:89
  117.1 1.7 copy-done.1
  118.8 2.6 fusion.4
  121.4 8.1 %fusion = bf16[4096,384]{0,1:T(8,128)(2,1)} fusion(bf16[1,384,4096]{2,1,0:T(8,128)(2,1)S(1)} %copy-done, bf16[384,4096]{1,0:T(8,128)(2,1)} %bitcast.124, bf16[1,4096,384]{2,1,0:T(8,128)(2,1)} %param.13, f32[384,384]{1,0:T(8,128)} %fusion.4), kind=kOutput, calls=%fused_computation.6 | convolution fusion | flops 2418376704 | bytes 13172736 | tf_op jit(solution)/shard_map/dot_general | solution.py:97
  129.5 0.2 reduce-scatter.7.cloned.1.call-start
  129.8 0.1 gather.22
  129.9 44.0 %reduce-scatter.5.cloned.1.call-done = bf16[512,48,8]{0,1,2:T(8,128)(2,1)} async-done(((bf16[4096,48,8]{0,1,2:T(8,128)(2,1)}), bf16[512,48,8]{0,1,2:T(8,128)(2,1)}) %reduce-scatter.5.cloned.1.call-update) | async-done | bytes 393232 | tf_op jit(solution)/shard_map/reduce_scatter | solution.py:20
  173.9 2.7 copy.58
  176.6 2.6 reshape.259
  179.3 0.1 reshape.229
  179.4 1.6 fusion.36
  181.0 1.4 gather_fusion.2
  182.4 0.1 reshape.238
  182.6 0.1 copy.51
  182.6 19.9 %reduce-scatter.7.cloned.1.call-done = bf16[128,384]{1,0:T(8,128)(2,1)} async-done(((bf16[512,384]{1,0:T(8,128)(2,1)}), bf16[128,384]{1,0:T(8,128)(2,1)}) %reduce-scatter.7.cloned.1.call-update) | async-done | bytes 98320
  202.5 1.1 reshape.260
  203.7 0.8 copy.59
  204.5 1.6 convert_element_type.49
  206.0 4.8 %all-to-all-start.1 = ((f32[128,48,8]{0,1,2:T(8,128)}), f32[128,48,8]{0,1,2:T(8,128)S(1)}, u32[]{:S(2)}, u32[]{:S(2)}) async-start(f32[128,48,8]{0,1,2:T(8,128)} %convert_element_type.49), calls=%async_computation.2 | async-start | bytes 393216 | tf_op jit(solution)/shard_map/all_to_all | solution.py:105
  210.8 5.3 %all-to-all-done.1 = f32[128,48,8]{0,1,2:T(8,128)S(1)} async-done(((f32[128,48,8]{0,1,2:T(8,128)}), f32[128,48,8]{0,1,2:T(8,128)S(1)}, u32[]{:S(2)}, u32[]{:S(2)}) %all-to-all-start.1) | async-done | bytes 196640 | tf_op jit(solution)/shard_map/all_to_all | solution.py:105
  216.2 0.7 gather_fusion.1
  216.9 0.9 fusion.28
  217.8 1.2 broadcast_in_dim.43
  219.0 8.4 %all-to-all-start.2 = ((bf16[32,128,128]{2,1,0:T(8,128)(2,1)}), bf16[32,128,128]{2,1,0:T(8,128)(2,1)}, u32[]{:S(2)}, u32[]{:S(2)}) async-start(bf16[32,128,128]{2,1,0:T(8,128)(2,1)} %broadcast_in_dim.43), calls=%async_computation.3 | async-start | bytes 2097152 | tf_op jit(solution)/shard_map/all_to_all | solution.py:32
  228.1 27.1 %all-to-all-done.2 = bf16[32,128,128]{2,1,0:T(8,128)(2,1)} async-done(((bf16[32,128,128]{2,1,0:T(8,128)(2,1)}), bf16[32,128,128]{2,1,0:T(8,128)(2,1)}, u32[]{:S(2)}, u32[]{:S(2)}) %all-to-all-start.2) | async-done | bytes 1048608 | tf_op jit(solution)/shard_map/all_to_all | solution.py:32
  255.2 3.8 %multiply_reduce_fusion = (f32[]{:T(128)}, f32[4096,128]{1,0:T(8,128)}) fusion(bf16[1,128,128]{2,1,0:T(8,128)(2,1)S(1)} %copy-done.3, bf16[32,128,128]{2,1,0:T(8,128)(2,1)} %all-to-all-done.2), kind=kOutput, calls=%fused_computation.13 | convolution fusion | flops 135266304 | bytes 3178500 | tf_op jit(solution)/shard_map/dot_general | solution.py:118
  259.0 1.3 broadcast_in_dim.45
  260.2 5.6 %all-to-all-start.3 = ((f32[32,1,1]{2,1,0:T(1,128)}), f32[32,1,1]{2,1,0:T(1,128)S(1)}, u32[]{:S(2)}, u32[]{:S(2)}) async-start(f32[32,1,1]{2,1,0:T(1,128)} %broadcast_in_dim.45), calls=%async_computation.4 | async-start | bytes 32768 | tf_op jit(solution)/shard_map/all_to_all | solution.py:32
  265.8 1.4 copy_bitcast_fusion
  267.2 2.3 fusion.13
  269.5 6.0 %all-to-all-done.3 = f32[32,1,1]{2,1,0:T(1,128)S(1)} async-done(((f32[32,1,1]{2,1,0:T(1,128)}), f32[32,1,1]{2,1,0:T(1,128)S(1)}, u32[]{:S(2)}, u32[]{:S(2)}) %all-to-all-start.3) | async-done | bytes 160 | tf_op jit(solution)/shard_map/all_to_all | solution.py:32
  275.5 0.6 reduce_sum.29
  276.9 2.7 fusion.14
  (27 shorter events, 0.3 us)
Async XLA Ops:
  7.2 114.2 %copy-start = (bf16[1,384,4096]{2,1,0:T(8,128)(2,1)S(1)}, bf16[1,384,4096]{2,1,0:T(8,128)(2,1)}, u32[]{:S(2)}) copy-start(bf16[1,384,4096]{2,1,0:T(8,128)(2,1)} %param.14) | copy-start | bytes 9437188
  7.2 55.5 %all-gather.2.cloned.1.call-start = ((), (), s32[]{:S(2)}) async-start(), calls=%async_computation.6 | async-start | bytes 1179648 | tf_op jit(solution)/shard_map/all_gather | solution.py:13
  21.8 152.1 %reduce-scatter.5.cloned.1.call-start = ((), (), s32[]{:S(2)}) async-start(), calls=%async_computation.7 | async-start | bytes 3538944 | tf_op jit(solution)/shard_map/reduce_scatter | solution.py:20
  74.7 44.1 %copy-start.5 = (bf16[1,4096,384]{2,1,0:T(8,128)(2,1)S(1)}, bf16[1,4096,384]{2,1,0:T(8,128)(2,1)}, u32[]{:S(2)}) copy-start(bf16[1,4096,384]{2,1,0:T(8,128)(2,1)} %param.12) | copy-start | bytes 9437188
  117.1 1.7 copy-start.1
  129.5 49.9 %copy-start.2 = (bf16[4096,8]{0,1:T(8,128)(2,1)S(1)}, bf16[4096,8]{0,1:T(8,128)(2,1)}, u32[]{:S(2)}) copy-start(bf16[4096,8]{0,1:T(8,128)(2,1)} %param.11) | copy-start | bytes 196612
  129.5 73.0 %reduce-scatter.7.cloned.1.call-start = ((), (), s32[]{:S(2)}) async-start(), calls=%async_computation.8 | async-start | bytes 491520
  181.0 1.6 copy-start.4
  206.0 10.1 %all-to-all-start.1 = ((f32[128,48,8]{0,1,2:T(8,128)}), f32[128,48,8]{0,1,2:T(8,128)S(1)}, u32[]{:S(2)}, u32[]{:S(2)}) async-start(f32[128,48,8]{0,1,2:T(8,128)} %convert_element_type.49), calls=%async_computation.2 | async-start | bytes 393216 | tf_op jit(solution)/shard_map/all_to_all | solution.py:105
  216.9 38.3 %copy-start.3 = (bf16[1,128,128]{2,1,0:T(8,128)(2,1)S(1)}, bf16[1,128,128]{2,1,0:T(8,128)(2,1)}, u32[]{:S(2)}) copy-start(bf16[1,128,128]{2,1,0:T(8,128)(2,1)} %param.16) | copy-start | bytes 98308
  219.0 36.2 %all-to-all-start.2 = ((bf16[32,128,128]{2,1,0:T(8,128)(2,1)}), bf16[32,128,128]{2,1,0:T(8,128)(2,1)}, u32[]{:S(2)}, u32[]{:S(2)}) async-start(bf16[32,128,128]{2,1,0:T(8,128)(2,1)} %broadcast_in_dim.43), calls=%async_computation.3 | async-start | bytes 2097152 | tf_op jit(solution)/shard_map/all_to_all | solution.py:32
  260.2 15.3 %all-to-all-start.3 = ((f32[32,1,1]{2,1,0:T(1,128)}), f32[32,1,1]{2,1,0:T(1,128)S(1)}, u32[]{:S(2)}, u32[]{:S(2)}) async-start(f32[32,1,1]{2,1,0:T(1,128)} %broadcast_in_dim.45), calls=%async_computation.4 | async-start | bytes 32768 | tf_op jit(solution)/shard_map/all_to_all | solution.py:32
Sparse Core Ops, SparseCore 0:
  21.9 40.6 all-gather.1
  129.6 44.1 reduce-scatter.4
  179.3 23.1 reduce-scatter.6
where the time goes:
time: 287 us; the launch traced here: 286 us
  waiting for transfers between devices  138 us (48%)
  blocking collectives  55.2 us (19%)
  local copies, waits for them, and re-layouts  33.8 us (12%)
  starting transfers between devices  19.1 us (7%)
  matrix products  18.4 us (6%)
  between operations  15.3 us (5%)
  other arithmetic  6.74 us (2%)
    reduce_scatter x1, waiting for transfers between devices, own_rows(): running = lax.psum_scatter(running, axis, scatter_dimension=0, tiled=True)  44 us
    all_to_all x1, blocking collectives, per_device(): lax.all_to_all(outgoing, 'expert', split_axis=0, concat_axis=0, tiled=True)  42.4 us
    all_gather x1, waiting for transfers between devices, gathered_by_axis(): out = lax.all_gather(out, axes[number], axis=dim, tiled=True)  35.2 us
    all_to_all x2, waiting for transfers between devices, from_everyone(): return lax.all_to_all(copies, axis, split_axis=0, concat_axis=0, tiled=True)  33.1 us
    unnamed x4, waiting for transfers between devices  19.9 us
    all_to_all x2, starting transfers between devices, from_everyone(): return lax.all_to_all(copies, axis, split_axis=0, concat_axis=0, tiled=True)  14 us
    all_gather x1, blocking collectives, gathered_by_axis(): out = lax.all_gather(out, axes[number], axis=dim, tiled=True)  12.8 us
    unnamed x18, local copies, waits for them, and re-layouts  10.7 us
  transfers between devices with their start and end apart: 6, of which 6 were waited for; matrix products, arithmetic and copies ran while one was open for 4% of the time, Pallas kernels for 0%

commit v1 on v0

v1 whole, which is shorter than its diff:
```python
import jax
import jax.numpy as jnp
from jax import lax
from jax.experimental import pallas as pl
from jax.experimental.pallas import tpu as pltpu
from jax.sharding import PartitionSpec as P

MESH = pl.DeviceIdType.MESH
BF = jnp.bfloat16
F32 = jnp.float32
NZ, NY = 8, 4
NF = NZ * NY
NE = 8
CAP = 48
TOK = 128
TF = TOK // NF
D = 4096
FD = 384
COL = 128
SLOTS = NE * CAP
R1 = 224
R2 = SLOTS - R1
Q1 = 80


def dot(a, b, dims=(((1,), (0,)), ((), ()))):
    return lax.dot_general(a, b, dims, preferred_element_type=F32)


def block(index):
    return pl.ds(pl.multiple_of(index * COL, COL), COL)


def add(*parts):
    total = parts[0].astype(F32)
    for part in parts[1:]:
        total = total + part.astype(F32)
    return total.astype(BF)


def kernel(
    tok_h, routes_h, router_h, gate_h, up_h, down_h, adapt_h, upstr_h, bound_ref,
    adapted_h, clipped_h,
    tok, routes, router, wg, wu, wd, adapt, upstr,
    xr, lr, ls, xf, lf, xc, a, ga, ua, pb, yb, ys, zb, z2, zs, w2, fin, rc, lay, grad, ns, nr, oa, oc,
    lsem, osem, a2a_s, a2a_r, log_s, log_r, pk_s, pk_r, rt_s, rt_r, nm_s, nm_r,
    ag_s, ag_r, rs_s, y_r, z_r, z2_r, w2_r, lg_s, lg_r,
):
    e = lax.axis_index("expert")
    f = lax.axis_index("ffn")
    z, y = f // NY, f % NY
    core = e % 2
    dm = 1 - 2 * core

    def zz(v):
        return (v + 2 * NZ) % NZ

    def yy(v):
        return (v + 2 * NY) % NY

    def at(zi, yi):
        return zi * NY + yi

    def sign(v):
        return 1 - 2 * ((v + core) % 2)

    def remote(src, dst, ss, rs, **where):
        return pltpu.make_async_remote_copy(
            src_ref=src, dst_ref=dst, send_sem=ss, recv_sem=rs,
            device_id=where, device_id_type=MESH,
        )

    loads = [
        pltpu.make_async_copy(src, dst, lsem.at[n])
        for n, (src, dst) in enumerate(
            ((tok_h, tok), (routes_h, routes), (router_h, router), (gate_h, wg), (up_h, wu),
             (down_h, wd), (upstr_h, upstr), (adapt_h, adapt))
        )
    ]
    for load in loads:
        load.start()

    barrier = pltpu.get_barrier_semaphore()

    @pl.loop(1, NF)
    def _(j):
        pl.semaphore_signal(barrier, inc=1, device_id={"ffn": (f + j) % NF}, device_id_type=MESH)

    @pl.loop(1, NE)
    def _(j):
        pl.semaphore_signal(barrier, inc=1, device_id={"expert": (e + j) % NE}, device_id_type=MESH)

    loads[0].wait()
    pl.semaphore_wait(barrier, NF - 1 + NE - 1)

    @pl.loop(1, NF)
    def _(j):
        peer = (f + j) % NF
        remote(tok.at[:, block(peer)], xr.at[f], a2a_s, a2a_r, ffn=peer).start()

    xr[f] = tok[:, block(f)]
    loads[2].wait()
    ls[...] = jnp.zeros_like(ls)
    ls[:, 0:NE] = dot(tok[...], router[...], (((1,), (1,)), ((), ())))

    @pl.loop(1, NF)
    def _(j):
        remote(ls, lr.at[f], log_s, log_r, ffn=(f + j) % NF).start()

    lr[f] = ls[...]

    loads[1].wait()
    r0, r1 = routes[0:1, :], routes[1:2, :]
    names = lax.broadcasted_iota(jnp.int32, (NE, TOK), 0)
    h0 = (names == r0).astype(F32)
    h1 = (names == r1).astype(F32)
    early = lax.broadcasted_iota(jnp.int32, (TOK, TOK), 0) < lax.broadcasted_iota(jnp.int32, (TOK, TOK), 1)
    before = dot((h0 + h1).astype(BF), early.astype(F32).astype(BF))
    slot0 = jnp.sum(before * h0, axis=0, keepdims=True).astype(jnp.int32) + r0 * CAP
    slot1 = jnp.sum(before * h1, axis=0, keepdims=True).astype(jnp.int32) + r1 * CAP
    places = lax.broadcasted_iota(jnp.int32, (SLOTS, TOK), 0)
    o0 = (places == slot0).astype(F32)
    o1 = (places == slot1).astype(F32)
    pick = (o0 + o1).astype(BF)

    others = pl.ds(0, NF - 1)
    remote(xr.at[others], xr.at[others], a2a_s, a2a_r, ffn=(f + 1) % NF).wait_recv()
    for n in range(NF):
        xf[TF * n:TF * (n + 1), :] = xr[n].astype(F32)
    xc[...] = dot(pick, xf[...].astype(BF)).astype(BF)

    mine = pl.ds(pl.multiple_of(e * CAP, CAP), CAP)

    @pl.loop(1, NE)
    def _(j):
        peer = (e + j) % NE
        theirs = pl.ds(pl.multiple_of(peer * CAP, CAP), CAP)
        remote(xc.at[theirs], a.at[mine, block(f)], pk_s, pk_r, expert=peer).start()

    a[mine, block(f)] = xc[mine, :]
    seven = pl.ds(0, CAP * (NE - 1))
    remote(xc.at[seven], rc.at[seven], pk_s, pk_r, expert=(e + 1) % NE).wait_recv()

    def gathered(buf, cut, total, ssem, rsem, on_chunk):
        sent = []
        rows = (pl.ds(0, cut), pl.ds(cut, total - cut))

        def piece(h, zi, yi, target):
            ref = buf.at[rows[h], block(at(zi, yi))]
            return remote(ref, ref, ssem.at[min(len(sent), 61)], rsem.at[h, at(zi, yi)], ffn=target)

        def send(h, zi, yi, zt, yt):
            copy = piece(h, zi, yi, at(zt, yt))
            copy.start()
            sent.append(copy)

        def wait(h, zi, yi):
            piece(h, zi, yi, at(zz(z + 1), y)).wait_recv()

        def to_y(h, zi, yi):
            send(h, zi, yi, z, yy(y + 1))
            send(h, zi, yi, z, yy(y - 1))

        def to_z(h, zi, yi):
            send(h, zi, yi, zz(z + 1), y)
            send(h, zi, yi, zz(z - 1), y)

        def first_z(k):
            def run():
                if k < 4:
                    for s in (1, -1):
                        wait(0, zz(z - s * k), y)
                        if k < 3:
                            send(0, zz(z - s * k), y, zz(z + s), y)
                    if k == 3:
                        send(0, zz(z - 3 * dm), y, zz(z + dm), y)
                    for s in (1, -1):
                        to_y(0, zz(z - s * k), y)
                else:
                    wait(0, zz(z + 4), y)
                    to_y(0, zz(z + 4), y)
            return run

        def then_y(off):
            def run():
                zi = zz(z + off)
                wait(0, zi, yy(y + 1))
                wait(0, zi, yy(y - 1))
                s = sign(zi)
                send(0, zi, yy(y - s), z, yy(y + s))
            return run

        def last_y(off):
            return lambda: wait(0, zz(z + off), yy(y + 2))

        def first_y(b):
            def run():
                wait(1, z, yy(y + b))
                to_z(1, z, yy(y + b))
            return run

        def then_z(b, k):
            def run():
                yi = yy(y + b)
                if k == 4:
                    wait(1, zz(z + 4), yi)
                    return
                for s in (1, -1):
                    wait(1, zz(z - s * k), yi)
                    if k < 3:
                        send(1, zz(z - s * k), yi, zz(z + s), y)
                if k == 3:
                    s = sign(yi)
                    send(1, zz(z - 3 * s), yi, zz(z + s), y)
            return run

        send(1, z, y, z, yy(y + 1))
        send(1, z, y, z, yy(y - 1))
        send(0, z, y, zz(z + 1), y)
        send(0, z, y, zz(z - 1), y)
        send(1, z, y, z, yy(y + 2))
        to_y(0, z, y)
        to_z(1, z, y)
        steps = [[] for _ in range(7)]
        for k in range(1, 5):
            steps[k].append(first_z(k))
        for b, r in ((1, 1), (-1, 1), (2, 2)):
            steps[r].append(first_y(b))
        for b, r in ((0, 0), (1, 1), (-1, 1), (2, 2)):
            for k in range(1, 5):
                steps[r + k].append(then_z(b, k))
        for off in (0, 1, -1, 2, -2, 3, -3, 4):
            steps[abs(off) + 1].append(then_y(off))
            steps[abs(off) + 2].append(last_y(off))
        for r in range(1, 7):
            for step in steps[r]:
                step()
            if r >= 2:
                for off in ((0,), (1, -1), (2, -2), (3, -3), (4,))[r - 2]:
                    on_chunk(zz(z + off), r == 2)
        for copy in sent:
            copy.wait_send()

    for n in (3, 4):
        loads[n].wait()

    def expert_chunk(zi, first):
        cols = pl.ds(pl.multiple_of(zi * NY * COL, NY * COL), NY * COL)
        x = a[:, cols]
        g, u = dot(x, wg[cols, :]), dot(x, wu[cols, :])
        if first:
            ga[...] = g
            ua[...] = u
        else:
            ga[...] += g
            ua[...] += u

    gathered(a, R1, SLOTS, ag_s, ag_r, expert_chunk)

    loads[5].wait()
    gate = ga[...]
    hidden = (gate / (1.0 + jnp.exp(-gate)) * ua[...]).astype(BF)

    @pl.loop(0, 8)
    def _(n):
        cols = pl.ds(pl.multiple_of(n * 512, 512), 512)
        pb[:, cols] = dot(hidden, wd[:, cols]).astype(BF)

    sent = []
    top, low = pl.ds(0, R1), pl.ds(R1, R2)

    def own(h, zi, yi):
        return pb.at[(top, low)[h], block(at(zi, yi))]

    def push(src, dst, rsem, zt, yt):
        copy = remote(src, dst, rs_s.at[len(sent)], rsem, ffn=at(zt, yt))
        copy.start()
        sent.append(copy)

    def got(dst, rsem):
        remote(dst, dst, rs_s.at[0], rsem, ffn=at(zz(z + 1), y)).wait_recv()

    offs = (4, 3 * dm, -3 * dm, 2 * dm, -2 * dm, dm, -dm, 0)

    def y1(i):
        zi = zz(z + offs[i])
        s = sign(zi)
        push(own(0, zi, yy(y + 2)), yb.at[i, 0], y_r.at[i, 0], z, yy(y + s))
        push(own(0, zi, yy(y - s)), yb.at[i, 2], y_r.at[i, 2], z, yy(y - s))

    def y2(i):
        zi = zz(z + offs[i])
        s = sign(zi)
        got(yb.at[i, 0], y_r.at[i, 0])
        yb[i, 0] = add(yb[i, 0], own(0, zi, yy(y + s))[...])
        push(yb.at[i, 0], yb.at[i, 1], y_r.at[i, 1], z, yy(y + s))

    def y3(i):
        zi = zz(z + offs[i])
        got(yb.at[i, 2], y_r.at[i, 2])
        got(yb.at[i, 1], y_r.at[i, 1])
        ys[i] = add(yb[i, 1], yb[i, 2], own(0, zi, y)[...])

    def z_first(i, slot, s):
        push(ys.at[i], zb.at[slot], z_r.at[slot], zz(z + s), y)

    def z_step(slot, i, to, s):
        got(zb.at[slot], z_r.at[slot])
        zb[slot] = add(zb[slot], ys[i])
        push(zb.at[slot], zb.at[to], z_r.at[to], zz(z + s), y)

    def z_last():
        got(zb.at[0], z_r.at[0])
        got(zb.at[4], z_r.at[4])
        fin[0:R1, :] = add(zb[0], zb[4], ys[7])

    boffs = (2, 1, -1, 0)

    def u1(j):
        yi = yy(y + boffs[j])
        s = sign(yi)
        push(own(1, zz(z + 4), yi), z2.at[j, 3], z2_r.at[j, 3], zz(z + s), y)
        push(own(1, zz(z - 3 * s), yi), z2.at[j, 6], z2_r.at[j, 6], zz(z - s), y)

    def u_step(j, r):
        yi = yy(y + boffs[j])
        s = sign(yi)
        k = 5 - r
        got(z2.at[j, k], z2_r.at[j, k])
        z2[j, k] = add(z2[j, k], own(1, zz(z + k * s), yi)[...])
        push(z2.at[j, k], z2.at[j, k - 1], z2_r.at[j, k - 1], zz(z + s), y)
        if k > 1:
            m = k - 1
            got(z2.at[j, 4 + m], z2_r.at[j, 4 + m])
            z2[j, 4 + m] = add(z2[j, 4 + m], own(1, zz(z - m * s), yi)[...])
            push(z2.at[j, 4 + m], z2.at[j, 3 + m], z2_r.at[j, 3 + m], zz(z - s), y)

    def u_last(j):
        yi = yy(y + boffs[j])
        got(z2.at[j, 0], z2_r.at[j, 0])
        got(z2.at[j, 4], z2_r.at[j, 4])
        zs[j] = add(z2[j, 0], z2[j, 4], own(1, z, yi)[...])
        if j < 3:
            push(zs.at[j], w2.at[j], w2_r.at[j], z, yi)

    def u_end():
        for j in range(3):
            got(w2.at[j], w2_r.at[j])
        fin[R1:SLOTS, :] = add(w2[0], w2[1], w2[2], zs[3])

    plan = []
    for i in range(8):
        plan.append((1.7 * (i - 1), lambda i=i: y1(i)))
        plan.append((1.84 * i + 3.2, lambda i=i: y2(i)))
        plan.append((1.84 * i + 6.2, lambda i=i: y3(i)))
    for when, run in (
        (6.5, lambda: z_first(0, 3, dm)),
        (9.9, lambda: z_first(2, 6, -dm)),
        (9.2, lambda: z_step(3, 1, 2, dm)),
        (12.2, lambda: z_step(2, 3, 1, dm)),
        (15.7, lambda: z_step(1, 5, 0, dm)),
        (13.9, lambda: z_step(6, 4, 5, -dm)),
        (17.5, lambda: z_step(5, 6, 4, -dm)),
        (20.0, z_last),
    ):
        plan.append((when, run))
    for j in range(4):
        plan.append((0.1 * j - 1.0, lambda j=j: u1(j)))
        for r in (2, 3, 4):
            plan.append((2.5 + 0.9 * j + 3.5 * (r - 2), lambda j=j, r=r: u_step(j, r)))
        plan.append((13.0 + 0.9 * j, lambda j=j: u_last(j)))
    plan.append((19.0, u_end))
    for _, run in sorted(plan, key=lambda item: item[0]):
        run()

    @pl.loop(1, NE)
    def _(j):
        peer = (e + j) % NE
        theirs = pl.ds(pl.multiple_of(peer * CAP, CAP), CAP)
        remote(fin.at[theirs], rc.at[mine], rt_s, rt_r, expert=peer).start()

    rc[mine, :] = fin[mine, :]
    remote(lr.at[others], lr.at[others], log_s, log_r, ffn=(f + 1) % NF).wait_recv()
    for n in range(NF):
        lf[TF * n:TF * (n + 1), :] = lr[n]
    logits = jnp.transpose(lf[...])[0:NE, :]
    gap = jnp.sum(logits * h0, axis=0, keepdims=True) - jnp.sum(logits * h1, axis=0, keepdims=True)
    weight0 = 1.0 / (1.0 + jnp.exp(-gap))
    share = o0 * weight0 + o1 * (1.0 - weight0)
    share_hi = share.astype(BF)
    share_lo = (share - share_hi.astype(F32)).astype(BF)
    first_dims = (((0,), (0,)), ((), ()))
    remote(fin.at[seven], rc.at[seven], rt_s, rt_r, expert=(e + 1) % NE).wait_recv()
    back = rc[...]
    mixture = dot(share_hi, back, first_dims) + dot(share_lo, back, first_dims)
    lay[:, block(f)] = (xf[...] + mixture).astype(BF)

    for n in (6, 7):
        loads[n].wait()
    oa_cols = []

    def adapter_chunk(zi, first):
        cols = pl.ds(pl.multiple_of(zi * NY * COL, NY * COL), NY * COL)
        x = lay[:, cols]
        g = dot(x, upstr[...], first_dims)
        grad[cols, :] = g
        part = jnp.sum((g * g).reshape(NY * COL // 8, 8, COL), axis=0)
        term = dot(x, adapt[cols, :])
        if first:
            ns[...] = part
            ga[0:TOK, 0:COL] = term
        else:
            ns[...] += part
            ga[0:TOK, 0:COL] += term

    gathered(lay, Q1, TOK, lg_s, lg_r, adapter_chunk)

    @pl.loop(1, NF)
    def _(j):
        remote(ns, nr.at[f], nm_s, nm_r, ffn=(f + j) % NF).start()

    nr[f] = ns[...]
    oa[...] = (lay[:, block(f)].astype(F32) + ga[0:TOK, 0:COL]).astype(BF)
    first_out = pltpu.make_async_copy(oa, adapted_h, osem.at[0])
    first_out.start()
    for copy in sent:
        copy.wait_send()
    remote(xr.at[others], xr.at[others], a2a_s, a2a_r, ffn=(f + 1) % NF).wait_send()
    remote(lr.at[others], lr.at[others], log_s, log_r, ffn=(f + 1) % NF).wait_send()
    remote(xc.at[seven], rc.at[seven], pk_s, pk_r, expert=(e + 1) % NE).wait_send()
    remote(fin.at[seven], rc.at[seven], rt_s, rt_r, expert=(e + 1) % NE).wait_send()
    norms = remote(nr.at[others], nr.at[others], nm_s, nm_r, ffn=(f + 1) % NF)
    norms.wait_recv()
    squared = jnp.sum(jnp.sum(nr[...], axis=0), keepdims=True)
    limit = bound_ref[0]
    factor = limit / jnp.maximum(jnp.sqrt(squared), limit)
    outs = []
    for n in range(4):
        part = slice(n * 1024, (n + 1) * 1024)
        oc[part, :] = (grad[part, :] * factor).astype(BF)
        out = pltpu.make_async_copy(oc.at[part, :], clipped_h.at[part, :], osem.at[1 + n])
        out.start()
        outs.append(out)
    norms.wait_send()
    first_out.wait()
    for out in outs:
        out.wait()


def per_device(tokens, routes, router, w_gate, w_up, w_down, adapter, upstream, bound):
    anywhere = pl.BlockSpec(memory_space=pl.ANY)
    vmem = pltpu.VMEM
    dma = pltpu.SemaphoreType.DMA
    adapted, clipped = pl.pallas_call(
        kernel,
        out_shape=(
            jax.ShapeDtypeStruct((TOK, COL), BF),
            jax.ShapeDtypeStruct((D, COL), BF),
        ),
        in_specs=[anywhere] * 8 + [pl.BlockSpec(memory_space=pltpu.SMEM)],
        out_specs=(anywhere, anywhere),
        scratch_shapes=[
            vmem((TF, D), BF), vmem((2, TOK), jnp.int32), vmem((NE, D), BF),
            vmem((D, FD), BF), vmem((D, FD), BF), vmem((FD, D), BF),
            vmem((D, COL), BF), vmem((TOK, COL), BF),
            vmem((NF, TF, COL), BF), vmem((NF, TF, COL), F32), vmem((TF, COL), F32),
            vmem((TOK, COL), F32), vmem((TOK, COL), F32),
            vmem((SLOTS, COL), BF), vmem((SLOTS, D), BF),
            vmem((SLOTS, FD), F32), vmem((SLOTS, FD), F32), vmem((SLOTS, D), BF),
            vmem((8, 3, R1, COL), BF), vmem((8, R1, COL), BF), vmem((7, R1, COL), BF),
            vmem((4, 7, R2, COL), BF), vmem((4, R2, COL), BF), vmem((3, R2, COL), BF),
            vmem((SLOTS, COL), BF), vmem((SLOTS, COL), BF),
            vmem((TOK, D), BF), vmem((D, COL), F32),
            vmem((8, COL), F32), vmem((NF, 8, COL), F32),
            vmem((TOK, COL), BF), vmem((D, COL), BF),
            dma((8,)), dma((5,)), dma, dma, dma, dma, dma, dma, dma, dma, dma, dma,
            dma((62,)), dma((2, NF)), dma((62,)), dma((8, 3)), dma((7,)), dma((4, 7)), dma((3,)),
            dma((62,)), dma((2, NF)),
        ],
        compiler_params=pltpu.CompilerParams(
            collective_id=0, has_side_effects=True, vmem_limit_bytes=60 * 1024 * 1024
        ),
    )(
        tokens[0], jnp.transpose(routes[0]), jnp.transpose(router), w_gate[0], w_up[0], w_down[0],
        adapter[0], upstream[0], bound,
    )
    return adapted[None], clipped[None]


def solution(mesh):
    placed = (
        P("expert", "ffn", None),
        P("expert", None, None),
        P(),
        P("expert", None, "ffn"),
        P("expert", None, "ffn"),
        P("expert", "ffn", None),
        P("expert", None, "ffn"),
        P("expert", None, "ffn"),
        P("expert"),
    )
    return jax.shard_map(
        per_device,
        mesh=mesh,
        in_specs=placed,
        out_specs=(P("expert", None, "ffn"), P("expert", None, "ffn")),
        check_vma=False,
    )
```

time: 287 us -> 121 us (0.42)
  waiting for transfers between devices: 138 us -> 0 us
  Pallas kernels: 0 us -> 115 us
  blocking collectives: 55.2 us -> 0 us
  local copies, waits for them, and re-layouts: 33.8 us -> 3.64 us
  starting transfers between devices: 19.1 us -> 0 us
  matrix products: 18.4 us -> 0 us
  between operations: 15.3 us -> 1.29 us
  other arithmetic: 6.74 us -> 0 us
    pallas_call x0 -> x1, Pallas kernels: none -> 115 us  [per_device(): pl.pallas_call(kernel, out_shape=(jax.ShapeDtypeStruct((TOK, COL), BF), j...]
    reduce_scatter x1 -> x0, waiting for transfers between devices: 44 us -> none  [own_rows(): running = lax.psum_scatter(running, axis, scatter_dimension=0, tiled=True)]
    all_to_all x1 -> x0, blocking collectives: 42.4 us -> none  [per_device(): lax.all_to_all(outgoing, 'expert', split_axis=0, concat_axis=0, tiled=True)]
    all_to_all x3 -> x0, waiting for transfers between devices: 38.5 us -> none  [the longest x2 33.1 us: from_everyone(): return lax.all_to_all(copies, axis, split_axis=0, concat_axis=0, tiled=True)]
    all_gather x1 -> x0, waiting for transfers between devices: 35.2 us -> none  [gathered_by_axis(): out = lax.all_gather(out, axes[number], axis=dim, tiled=True)]
    unnamed x4 -> x0, waiting for transfers between devices: 19.9 us -> none
    all_to_all x3 -> x0, starting transfers between devices: 18.8 us -> none  [the longest x2 14 us: from_everyone(): return lax.all_to_all(copies, axis, split_axis=0, concat_axis=0, tiled=True)]
    dot_general x5 -> x0, matrix products: 18.4 us -> none  [the longest x1 8.14 us: per_device(): lax.dot_general(down_cols, hidden, (((0,), (1,)), ((), ())), preferred_el...]
  transfers between devices with their start and end apart: 6 -> 0, of which waited for: 6 -> 0; matrix products, arithmetic and copies ran while one was open for 4% -> 0% of each run, Pallas kernels for 0% -> 0%
where the time goes in v1:
time: 121 us; the launch traced here: 120 us
  Pallas kernels  115 us (95%)
  local copies, waits for them, and re-layouts  3.64 us (3%)
  between operations  1.29 us (1%)
    pallas_call x1, Pallas kernels, per_device(): pl.pallas_call(kernel, out_shape=(jax.ShapeDtypeStruct((TOK, COL), BF), j...  115 us
    unnamed x2, local copies, waits for them, and re-layouts  3.64 us

profile of v1, /device:TPU:2, one launch (start us, length us, event | category | flops | bytes accessed | tf_op | source)
XLA Modules:
  0.0 120.1 jit_solution(17541919212981524604)
XLA Ops:
  1.3 115.1 %shard_map.104 = (bf16[128,128]{1,0:T(8,128)(2,1)}, bf16[4096,128]{1,0:T(8,128)(2,1)}) custom-call(bf16[4,4096]{1,0:T(4,128)(2,1)} %bitcast.18, s32[2,128]{1,0:T(2,128)} %bitcast.21, bf16[8,4096]{1,0:T(8,128)(2,1)} %bitcast.17, bf16[4096,384]{1,0:T(8,128)(2,1)} %bitcast.12, bf16[4096,384]{1,0:T(8,128)(2,1)} %bitcast.13, bf16[384,4096]{1,0:T(8,128)(2,1)} %bitcast.14, ...), custom_call_target="tpu_custom_call" | custom-call | tf_op jit(solution)/shard_map/pallas_call | solution.py:454
  116.4 1.4 %copy.14 = bf16[1,128,128]{2,1,0:T(8,128)(2,1)} copy(bf16[1,128,128]{2,1,0:T(8,128)(2,1)} %bitcast.20) | data formatting | bytes 65536
  117.8 2.3 %copy.15 = bf16[1,4096,128]{2,1,0:T(8,128)(2,1)} copy(bf16[1,4096,128]{2,1,0:T(8,128)(2,1)} %bitcast.15) | data formatting | bytes 2097152

commit v2 on v0

v2 whole, which is shorter than its diff:
```python
import jax
import jax.numpy as jnp
from jax import lax
from jax.experimental import pallas as pl
from jax.experimental.pallas import tpu as pltpu
from jax.sharding import PartitionSpec as P

MESH = pl.DeviceIdType.MESH
BF = jnp.bfloat16
F32 = jnp.float32
NZ, NY = 8, 4
NF = NZ * NY
NE = 8
CAP = 48
TOK = 128
TF = TOK // NF
D = 4096
FD = 384
COL = 128
SLOTS = NE * CAP
GROUPS = (((0, 240, 1, True), (240, 144, 2, False)),)
WIDE = ((0, 80, 1, True), (80, 48, 2, True))
PARTS = tuple(part for group in GROUPS for part in group)
RATE = 46.6e3
FIRST_HOP, NEXT_HOP, LEAD = 2.2, 0.75, 0.8
BIAS, U_BIAS = (0.0, 0.0), 0.0


def dot(a, b, dims=(((1,), (0,)), ((), ()))):
    return lax.dot_general(a, b, dims, preferred_element_type=F32)


def block(index):
    return pl.ds(pl.multiple_of(index * COL, COL), COL)


def add(*parts):
    total = parts[0].astype(F32)
    for part in parts[1:]:
        total = total + part.astype(F32)
    return total.astype(BF)


def parity(v):
    return 1 if v % 2 == 0 else -1


def spread(kind, skip):
    out = []

    def along(b, s0):
        for s in (1, -1):
            out.append((0, b, s, 0))
            if skip:
                out.append((0, b, 2 * s, 0))
                out.append((-2 * s, b, s, 0))
                if s == s0:
                    out.append((-2 * s, b, 2 * s, 0))
            else:
                out.append((-s, b, s, 0))
                out.append((-2 * s, b, s, 0))
                if s == s0:
                    out.append((-3 * s, b, s, 0))

    if kind == 1:
        along(0, 1)
        for a in range(-3, 5):
            sg = parity(a)
            out.extend(((a, 0, 0, 1), (a, 0, 0, -1), (a, -sg, 0, sg)))
    else:
        out.extend(((0, 0, 0, 1), (0, 0, 0, -1), (0, 0, 0, 2)))
        for b in range(-1, 3):
            along(b, parity(b))
    return out


def wrap(a, b):
    return (a + 3) % 8 - 3, (b + 1) % 4 - 1


class Plan:
    def __init__(self):
        self.nodes = []
        self.waits = {}
        self.given = {}
        self.bias = 0.0

    def send(self, needs, makes, link, size, hops, act, wait, work=0.02):
        self.nodes.append(dict(needs=needs, makes=makes, link=link, cost=size / RATE, hops=hops, act=act, work=work, bias=self.bias))
        self.waits[makes] = wait

    def post(self, needs, makes, delay, act, wait, work=0.1):
        self.nodes.append(dict(needs=needs, makes=makes, link=None, delay=delay, act=act, work=work, bias=self.bias))
        self.waits[makes] = wait

    def compute(self, needs, makes, work, act):
        self.nodes.append(dict(needs=needs, makes=makes, link=None, delay=0.0, act=act, work=work, bias=self.bias))

    def order(self):
        users = {}
        for node in self.nodes:
            for need in node["needs"]:
                users.setdefault(need, []).append(node)
        length = {}

        def path(node):
            key = id(node)
            if key not in length:
                if node["link"] is None:
                    own = node["work"] + node["delay"]
                else:
                    own = node["work"] + node["cost"] * node["hops"] + FIRST_HOP + NEXT_HOP * (node["hops"] - 1)
                length[key] = own + max([path(user) for user in users.get(node["makes"], ())] or [0.0])
            return length[key]

        for node in self.nodes:
            path(node)
        known, free, core, busy, out = dict(self.given), {}, 0.0, (0.0, 0.0), []
        pending = list(self.nodes)
        while pending:
            best = None
            for at, node in enumerate(pending):
                if any(need not in known for need in node["needs"]):
                    continue
                ready = max([known[need] for need in node["needs"]] or [0.0])
                if node["link"] is None:
                    start = max(ready, core)
                else:
                    if busy[0] < ready < busy[1]:
                        ready = busy[1]
                    start = max(ready, free.get(node["link"], 0.0))
                key = (round(start, 2), node["link"] is None and node["work"] > 0.15, -length[id(node)] - node["bias"], at)
                if best is None or key < best[0]:
                    best = (key, node, ready, start)
            _, node, ready, start = best
            pending.remove(node)
            if node["link"] is None:
                core = start + node["work"]
                busy = (start, core)
                known[node["makes"]] = core + node["delay"]
                out.append((start, len(out), node))
            else:
                free[node["link"]] = start + node["cost"] * node["hops"]
                known[node["makes"]] = start + node["work"] + node["cost"] + FIRST_HOP + NEXT_HOP * (node["hops"] - 1)
                out.append((max(ready, start - LEAD), len(out), node))
        return [node for _, _, node in sorted(out, key=lambda item: item[:2])], max(known.values())

    def emit(self):
        order, _ = self.order()
        waited = set()
        for node in order:
            for need in node["needs"]:
                if need in self.waits and need not in waited:
                    waited.add(need)
                    self.waits[need]()
            node["act"]()
        for need, wait in self.waits.items():
            if need not in waited:
                wait()


def kernel(
    tok_h, routes_h, router_h, gate_h, up_h, down_h, adapt_h, upstr_h, bound_ref,
    adapted_h, clipped_h,
    tok, routes, router, wg, wu, wd, adapt, xr, lr, ls, xf, lf, xc, a, ga, ua, hid, pb, *rest,
):
    bufs, rest = rest[:len(PARTS)], rest[len(PARTS):]
    (fin, rc, lay, ups, acc, ones, ns, nr, factor, oa, oc,
     lsem, osem, a2a_s, a2a_r, log_s, log_r, pk_s, pk_r, rt_s, rt_r, nm_s, nm_r,
     ag_s, ag_r, rs_s, rs_r, lg_s, lg_r, ug_s, ug_r) = rest
    e = lax.axis_index("expert")
    f = lax.axis_index("ffn")
    z, y = f // NY, f % NY
    core = e % 2
    turn_z = {1: 1 - 2 * core, 2: 1 - 2 * ((y + core) % 2)}
    turn_y = {1: 1 - 2 * ((z + core) % 2), 2: 1}
    first_dims = (((0,), (0,)), ((), ()))

    def spot(kind, da, db):
        zi = (z + turn_z[kind] * da + 2 * NZ) % NZ
        yi = (y + turn_y[kind] * db + 2 * NY) % NY
        return zi * NY + yi

    def remote(src, dst, ss, rs, **where):
        return pltpu.make_async_remote_copy(
            src_ref=src, dst_ref=dst, send_sem=ss, recv_sem=rs,
            device_id=where, device_id_type=MESH,
        )

    def towards(da, db):
        return ("z", da > 0) if da else ("y", db > 0)

    loads = [
        pltpu.make_async_copy(src, dst, lsem.at[n])
        for n, (src, dst) in enumerate(
            ((tok_h, tok), (routes_h, routes), (router_h, router), (upstr_h, ups.at[:, block(f)]),
             (gate_h, wg), (up_h, wu), (down_h, wd), (adapt_h, adapt))
        )
    ]
    for load in loads:
        load.start()

    barrier = pltpu.get_barrier_semaphore()

    @pl.loop(1, NF)
    def _(j):
        pl.semaphore_signal(barrier, inc=1, device_id={"ffn": (f + j) % NF}, device_id_type=MESH)

    @pl.loop(1, NE)
    def _(j):
        pl.semaphore_signal(barrier, inc=1, device_id={"expert": (e + j) % NE}, device_id_type=MESH)

    loads[0].wait()
    pl.semaphore_wait(barrier, NF - 1 + NE - 1)

    plan = Plan()
    others = pl.ds(0, NF - 1)
    seven = pl.ds(0, CAP * (NE - 1))
    mine = pl.ds(pl.multiple_of(e * CAP, CAP), CAP)
    next_f, next_e = (f + 1) % NF, (e + 1) % NE

    def loaded(n):
        plan.waits["load", n] = loads[n].wait
        plan.given["load", n] = 0.0
        return "load", n

    def to_columns():
        @pl.loop(1, NF)
        def _(j):
            peer = (f + j) % NF
            remote(tok.at[:, block(peer)], xr.at[f], a2a_s, a2a_r, ffn=peer).start()

        xr[f] = tok[:, block(f)]

    columns = remote(xr.at[others], xr.at[others], a2a_s, a2a_r, ffn=next_f)
    plan.post([], "columns", 4.6, to_columns, columns.wait_recv, 0.2)

    def own_logits():
        loads[2].wait()
        ls[...] = jnp.zeros_like(ls)
        ls[:, 0:NE] = dot(tok[...], router[...], (((1,), (1,)), ((), ())))

        @pl.loop(1, NF)
        def _(j):
            remote(ls, lr.at[f], log_s, log_r, ffn=(f + j) % NF).start()

        lr[f] = ls[...]

    everyone = remote(lr.at[others], lr.at[others], log_s, log_r, ffn=next_f)
    plan.post([], "logits", 6.0, own_logits, everyone.wait_recv, 0.55)

    def own_slots():
        loads[1].wait()
        r0, r1 = routes[0:1, :], routes[1:2, :]
        names = lax.broadcasted_iota(jnp.int32, (NE, TOK), 0)
        h0 = (names == r0).astype(F32)
        h1 = (names == r1).astype(F32)
        early = lax.broadcasted_iota(jnp.int32, (TOK, TOK), 0) < lax.broadcasted_iota(jnp.int32, (TOK, TOK), 1)
        before = dot((h0 + h1).astype(BF), early.astype(F32).astype(BF))
        slot0 = jnp.sum(before * h0, axis=0, keepdims=True).astype(jnp.int32) + r0 * CAP
        slot1 = jnp.sum(before * h1, axis=0, keepdims=True).astype(jnp.int32) + r1 * CAP
        places = lax.broadcasted_iota(jnp.int32, (SLOTS, TOK), 0)
        ones[0] = (places == slot0).astype(F32)
        ones[1] = (places == slot1).astype(F32)

    plan.compute([], "slots", 0.2, own_slots)

    def pack():
        for n in range(NF):
            xf[TF * n:TF * (n + 1), :] = xr[n].astype(F32)
        xc[...] = dot((ones[0] + ones[1]).astype(BF), xf[...].astype(BF)).astype(BF)

        @pl.loop(1, NE)
        def _(j):
            peer = (e + j) % NE
            theirs = pl.ds(pl.multiple_of(peer * CAP, CAP), CAP)
            remote(xc.at[theirs], a.at[mine, block(f)], pk_s, pk_r, expert=peer).start()

        a[mine, block(f)] = xc[mine, :]

    packed = remote(xc.at[seven], rc.at[seven], pk_s, pk_r, expert=next_e)
    plan.post(["columns", "slots"], "packed", 4.3, pack, packed.wait_recv, 0.2)

    def gather(name, buf, parts, ssem, rsem, start, chunk_work, on_chunk, extra=(), before=()):
        pieces = {}
        for p, (row, rows, kind, skip) in enumerate(parts):
            for da, db, sa, sb in spread(kind, skip):
                def act(p=p, row=row, rows=rows, kind=kind, da=da, db=db, sa=sa, sb=sb):
                    ref = buf.at[pl.ds(row, rows), block(spot(kind, da, db))]
                    remote(ref, ref, ssem.at[p], rsem.at[p, spot(kind, da, db)], ffn=spot(kind, sa, sb)).start()

                ra, rb = wrap(da - sa, db - sb)

                def wait(p=p, row=row, rows=rows, kind=kind, ra=ra, rb=rb):
                    ref = buf.at[pl.ds(row, rows), block(spot(kind, ra, rb))]
                    remote(ref, ref, ssem.at[p], rsem.at[p, spot(kind, ra, rb)], ffn=next_f).wait_recv()

                held = (name, p, da, db) if (da, db) != (0, 0) else start
                makes = (name, p, ra, rb)
                pieces.setdefault(abs(ra), []).append(makes)
                plan.send([held, *before], makes, towards(sa, sb), rows * COL * 2, abs(sa) + abs(sb), act, wait)
        for k in range(5):
            for s in ((1,) if k in (0, 4) else (1, -1)):
                needs = [start, *pieces[k], *extra]
                if k:
                    needs.append((name, "chunk", 0, 1))
                plan.compute(needs, (name, "chunk", k, s), chunk_work,
                             lambda k=k, s=s: on_chunk((z + s * k + NZ) % NZ, k == 0))
        return [(name, "chunk", k, s) for k in range(5) for s in ((1,) if k in (0, 4) else (1, -1))]

    def gather_done(buf, parts, ssem):
        for p, (row, rows, _, _) in enumerate(parts):
            ref = buf.at[pl.ds(row, rows), pl.ds(0, COL * (NF - 1))]
            remote(ref, ref, ssem.at[p], lg_r.at[0, 0], ffn=next_f).wait_send()

    plan.bias = U_BIAS
    ups_all = gather("u", ups, WIDE, ug_s, ug_r, loaded(3), 0.0, lambda zi, first: None)

    fins = []
    for g, group in enumerate(GROUPS):
        base, size = group[0][0], sum(part[1] for part in group)
        span = pl.ds(base, size)
        plan.bias = BIAS[g]

        def expert_chunk(zi, first, span=span):
            cols = pl.ds(pl.multiple_of(zi * NY * COL, NY * COL), NY * COL)
            x = a[span, cols]
            left, right = dot(x, wg[cols, :]), dot(x, wu[cols, :])
            if first:
                ga[span, :] = left
                ua[span, :] = right
            else:
                ga[span, :] += left
                ua[span, :] += right

        sub = [ag_s.at[pl.ds(2 * g, 2)], ag_r.at[pl.ds(2 * g, 2)]]
        chunks = gather(("x", g), a, group, *sub, "packed", 0.45 * size / SLOTS + 0.05, expert_chunk,
                        (loaded(4), loaded(5)))

        def hide(span=span):
            gate = ga[span, :]
            hid[span, :] = (gate / (1.0 + jnp.exp(-gate)) * ua[span, :]).astype(BF)

        plan.compute(chunks, ("hid", g), 0.5 * size / SLOTS, hide)
        for k in (4, 3, 2, 1, 0):
            def down(k=k, span=span):
                for s in ((1,) if k in (0, 4) else (1, -1)):
                    zi = (z + s * k + NZ) % NZ
                    cols = pl.ds(pl.multiple_of(zi * NY * COL, NY * COL), NY * COL)
                    pb[span, cols] = dot(hid[span, :], wd[:, cols]).astype(BF)

            plan.compute([("hid", g), loaded(6)], ("pb", g, k), (0.3 if k in (0, 4) else 0.6) * size / SLOTS, down)

        for p, (row, rows, kind, skip) in enumerate(group):
            buf, q = bufs[2 * g + p], 2 * g + p
            slots = {}

            def slot(key, slots=slots):
                return slots.setdefault(key, len(slots))

            def own(da, db, row=row, rows=rows, kind=kind):
                return pb.at[pl.ds(row, rows), block(spot(kind, da, db))]

            def hop(key, needs, parts, sa, sb, buf=buf, q=q, kind=kind, rows=rows, slot=slot):
                to = slot(key)

                def act():
                    refs = [part() for part in parts]
                    if len(refs) > 1:
                        refs[0][...] = add(*[ref[...] for ref in refs])
                    remote(refs[0], buf.at[to], rs_s.at[q], rs_r.at[q, to], ffn=spot(kind, sa, sb)).start()

                def wait():
                    remote(buf.at[to], buf.at[to], rs_s.at[q], rs_r.at[q, to], ffn=next_f).wait_recv()

                plan.send(needs, (q, key), towards(sa, sb), rows * COL * 2, abs(sa) + abs(sb), act, wait,
                          0.02 if len(parts) == 1 else 0.08)

            def here(key, buf=buf, slot=slot):
                return lambda: buf.at[slot(key)]

            def total(makes, needs, parts, out, q=q):
                def act():
                    out()[...] = add(*[part()[...] for part in parts])

                plan.compute(needs, makes, 0.1, act)

            def mid(n, buf=buf):
                return lambda: buf.at[31 + n]

            def mine_at(da, db, own=own):
                return lambda: own(da, db)

            done = ("fin", q)
            final = lambda row=row, rows=rows: fin.at[pl.ds(row, rows), :]
            if kind == 1:
                for da in range(-3, 5):
                    sg, ready = parity(da), ("pb", g, abs(da))
                    hop(("y0", da), [ready], [mine_at(da, 2)], 0, sg)
                    hop(("y2", da), [ready], [mine_at(da, -sg)], 0, -sg)
                    hop(("y1", da), [ready, (q, ("y0", da))], [here(("y0", da)), mine_at(da, sg)], 0, sg)
                    total((q, "sum", da), [ready, (q, ("y1", da)), (q, ("y2", da))],
                          [here(("y1", da)), here(("y2", da)), mine_at(da, 0)], mid(da + 3))
                for s in (1, -1):
                    far = [(q, ("z3", s))] + ([(q, ("z4", s))] if s == 1 else [])
                    if s == 1:
                        hop(("z4", s), [(q, "sum", 4)], [mid(7)], 2, 0)
                    hop(("z3", s), [(q, "sum", 3 * s)], [mid(3 * s + 3)], s, 0)
                    hop(("z2", s), [(q, "sum", 2 * s), *far],
                        [here(("z3", s)), mid(2 * s + 3)] + ([here(("z4", s))] if s == 1 else []), 2 * s, 0)
                    hop(("z1", s), [(q, "sum", s)], [mid(s + 3)], s, 0)
                ends = [("z2", 1), ("z2", -1), ("z1", 1), ("z1", -1)]
                total(done, [(q, "sum", 0)] + [(q, end) for end in ends], [mid(3)] + [here(end) for end in ends], final)
            else:
                for db in range(-1, 3):
                    for s in (1, -1):
                        last = 4 if s == parity(db) else 3
                        for k in range(last, 0, -1):
                            ready = ("pb", g, k)
                            if k == last:
                                hop(("v", db, s, k - 1), [ready], [mine_at(s * k, db)], s, 0)
                            else:
                                hop(("v", db, s, k - 1), [ready, (q, ("v", db, s, k))],
                                    [here(("v", db, s, k)), mine_at(s * k, db)], s, 0)
                    total((q, "sum", db), [("pb", g, 0), (q, ("v", db, 1, 0)), (q, ("v", db, -1, 0))],
                          [mine_at(0, db), here(("v", db, 1, 0)), here(("v", db, -1, 0))], mid(db + 1))
                    if db:
                        hop(("w", db), [(q, "sum", db)], [mid(db + 1)], 0, db)
                total(done, [(q, "sum", 0)] + [(q, ("w", db)) for db in (1, -1, 2)],
                      [mid(1)] + [here(("w", db)) for db in (1, -1, 2)], final)
            fins.append(done)

    plan.bias = 0.0

    def give_back():
        @pl.loop(1, NE)
        def _(j):
            peer = (e + j) % NE
            theirs = pl.ds(pl.multiple_of(peer * CAP, CAP), CAP)
            remote(fin.at[theirs], rc.at[mine], rt_s, rt_r, expert=peer).start()

        rc[mine, :] = fin[mine, :]

    returned = remote(fin.at[seven], rc.at[seven], rt_s, rt_r, expert=next_e)
    plan.post(fins, "back", 4.3, give_back, returned.wait_recv, 0.1)

    def weigh():
        for n in range(NF):
            lf[TF * n:TF * (n + 1), :] = lr[n]
        logits = jnp.transpose(lf[...])[0:NE, :]
        names = lax.broadcasted_iota(jnp.int32, (NE, TOK), 0)
        gap = jnp.sum(logits * (names == routes[0:1, :]).astype(F32), axis=0, keepdims=True)
        gap = gap - jnp.sum(logits * (names == routes[1:2, :]).astype(F32), axis=0, keepdims=True)
        weight0 = 1.0 / (1.0 + jnp.exp(-gap))
        ones[0] = ones[0] * weight0 + ones[1] * (1.0 - weight0)

    plan.compute(["logits", "packed"], "share", 0.5, weigh)

    def combine():
        share = ones[0]
        share_hi = share.astype(BF)
        share_lo = (share - share_hi.astype(F32)).astype(BF)
        back = rc[...]
        mixture = dot(share_hi, back, first_dims) + dot(share_lo, back, first_dims)
        lay[:, block(f)] = (xf[...] + mixture).astype(BF)

    plan.compute(["back", "share"], "layer", 0.3, combine)

    def square():
        own_t = jnp.transpose(lay[:, block(f)].astype(F32)).astype(BF)
        total = jnp.zeros((TOK, COL), F32)
        for n in range(NZ):
            part = dot(own_t, ups[:, n * NY * COL:(n + 1) * NY * COL])
            part = part * part
            total = total + (part[:, 0:128] + part[:, 128:256]) + (part[:, 256:384] + part[:, 384:512])
        ns[...] = jnp.sum(total.reshape(16, 8, COL), axis=0)

        @pl.loop(1, NF)
        def _(j):
            remote(ns, nr.at[f], nm_s, nm_r, ffn=(f + j) % NF).start()

        nr[f] = ns[...]

    norms = remote(nr.at[others], nr.at[others], nm_s, nm_r, ffn=next_f)
    plan.post(["layer", ("early", 0), *ups_all], "norms", 6.0, square, norms.wait_recv, 0.6)

    def scale():
        squared = jnp.sum(jnp.sum(nr[...], axis=0), keepdims=True)
        limit = bound_ref[0]
        factor[...] = jnp.broadcast_to(limit / jnp.maximum(jnp.sqrt(squared), limit), (8, COL))

    plan.compute(["norms"], "factor", 0.2, scale)
    outs = []

    def adapter_chunk(zi, first):
        cols = pl.ds(pl.multiple_of(zi * NY * COL, NY * COL), NY * COL)
        x = lay[:, cols]
        grad = dot(x, ups[:, block(f)], first_dims)
        oc[cols, :] = (grad * factor[0:1, :]).astype(BF)
        out = pltpu.make_async_copy(oc.at[cols, :], clipped_h.at[cols, :], osem.at[1 + len(outs)])
        out.start()
        outs.append(out)
        term = dot(x, adapt[cols, :])
        if first:
            acc[...] = term
        else:
            acc[...] += term

    plan.compute(["layer"], ("early", 0), 0.01, lambda: None)
    gather("l", lay, WIDE, lg_s, lg_r, "layer", 0.16, adapter_chunk, ("factor", loaded(7)))
    plan.emit()

    oa[...] = (lay[:, block(f)].astype(F32) + acc[...]).astype(BF)
    first_out = pltpu.make_async_copy(oa, adapted_h, osem.at[0])
    first_out.start()
    columns.wait_send()
    everyone.wait_send()
    packed.wait_send()
    returned.wait_send()
    norms.wait_send()
    gather_done(ups, WIDE, ug_s)
    gather_done(lay, WIDE, lg_s)
    gather_done(a, PARTS, ag_s)
    for q, (_, rows, _, _) in enumerate(PARTS):
        ref = bufs[q].at[pl.ds(0, NF - 1)]
        remote(ref, ref, rs_s.at[q], rs_r.at[q, 0], ffn=next_f).wait_send()
    first_out.wait()
    for out in outs:
        out.wait()


def pass_on(adapted_h, clipped_h, adapted_out, clipped_out, held, small, sem_in, sem_out):
    steps = [(adapted_h, small, adapted_out)]
    for n in range(4):
        part = pl.ds(n * D // 4, D // 4)
        steps.append((clipped_h.at[part, :], held.at[part, :], clipped_out.at[part, :]))
    ins = [pltpu.make_async_copy(src, mid, sem_in.at[n]) for n, (src, mid, _) in enumerate(steps)]
    outs = [pltpu.make_async_copy(mid, dst, sem_out.at[n]) for n, (_, mid, dst) in enumerate(steps)]
    for copy in ins:
        copy.start()
    for copy, out in zip(ins, outs):
        copy.wait()
        out.start()
    for out in outs:
        out.wait()


def per_device(tokens, routes, router, w_gate, w_up, w_down, adapter, upstream, bound):
    anywhere = pl.BlockSpec(memory_space=pl.ANY)
    vmem = pltpu.VMEM
    dma = pltpu.SemaphoreType.DMA
    adapted, clipped = pl.pallas_call(
        kernel,
        out_shape=(
            jax.ShapeDtypeStruct((TOK, COL), BF),
            jax.ShapeDtypeStruct((D, COL), BF),
        ),
        in_specs=[anywhere] * 8 + [pl.BlockSpec(memory_space=pltpu.SMEM)],
        out_specs=(anywhere, anywhere),
        scratch_shapes=[
            vmem((TF, D), BF), vmem((2, TOK), jnp.int32), vmem((NE, D), BF),
            vmem((D, FD), BF), vmem((D, FD), BF), vmem((FD, D), BF), vmem((D, COL), BF),
            vmem((NF, TF, COL), BF), vmem((NF, TF, COL), F32), vmem((TF, COL), F32),
            vmem((TOK, COL), F32), vmem((TOK, COL), F32),
            vmem((SLOTS, COL), BF), vmem((SLOTS, D), BF),
            vmem((SLOTS, FD), F32), vmem((SLOTS, FD), F32), vmem((SLOTS, FD), BF), vmem((SLOTS, D), BF),
            *[vmem((39, part[1], COL), BF) for part in PARTS],
            vmem((SLOTS, COL), BF), vmem((SLOTS, COL), BF),
            vmem((TOK, D), BF), vmem((TOK, D), BF), vmem((TOK, COL), F32), vmem((2, SLOTS, TOK), F32),
            vmem((8, COL), F32), vmem((NF, 8, COL), F32), vmem((8, COL), F32),
            vmem((TOK, COL), BF), vmem((D, COL), BF),
            dma((8,)), dma((9,)), dma, dma, dma, dma, dma, dma, dma, dma, dma, dma,
            dma((len(PARTS),)), dma((len(PARTS), NF)), dma((len(PARTS),)), dma((len(PARTS), NF - 1)),
            dma((2,)), dma((2, NF)), dma((2,)), dma((2, NF)),
        ],
        compiler_params=pltpu.CompilerParams(
            collective_id=0, has_side_effects=True, vmem_limit_bytes=60 * 1024 * 1024
        ),
    )(
        tokens[0], jnp.transpose(routes[0]), jnp.transpose(router), w_gate[0], w_up[0], w_down[0],
        adapter[0], upstream[0], bound,
    )
    shapes = (jax.ShapeDtypeStruct((TOK, COL), BF), jax.ShapeDtypeStruct((D, COL), BF))
    adapted, clipped = pl.pallas_call(
        pass_on,
        out_shape=shapes,
        in_specs=[anywhere] * 2,
        out_specs=(anywhere, anywhere),
        scratch_shapes=[vmem((D, COL), BF), vmem((TOK, COL), BF), dma((5,)), dma((5,))],
    )(adapted, clipped)
    return adapted[None], clipped[None]


def solution(mesh):
    placed = (
        P("expert", "ffn", None),
        P("expert", None, None),
        P(),
        P("expert", None, "ffn"),
        P("expert", None, "ffn"),
        P("expert", "ffn", None),
        P("expert", None, "ffn"),
        P("expert", None, "ffn"),
        P("expert"),
    )
    return jax.shard_map(
        per_device,
        mesh=mesh,
        in_specs=placed,
        out_specs=(P("expert", None, "ffn"), P("expert", None, "ffn")),
        check_vma=False,
    )
```

time: 287 us -> 96.3 us (0.34)
  waiting for transfers between devices: 138 us -> 0 us
  Pallas kernels: 0 us -> 94 us
  blocking collectives: 55.2 us -> 0 us
  local copies, waits for them, and re-layouts: 33.8 us -> 0 us
  starting transfers between devices: 19.1 us -> 0 us
  matrix products: 18.4 us -> 0 us
  between operations: 15.3 us -> 1.29 us
  other arithmetic: 6.74 us -> 0 us
    pallas_call x0 -> x2, Pallas kernels: none -> 94 us  [the longest x1 92 us: per_device(): pl.pallas_call(kernel, out_shape=(jax.ShapeDtypeStruct((TOK, COL), BF), j...]
    reduce_scatter x1 -> x0, waiting for transfers between devices: 44 us -> none  [own_rows(): running = lax.psum_scatter(running, axis, scatter_dimension=0, tiled=True)]
    all_to_all x1 -> x0, blocking collectives: 42.4 us -> none  [per_device(): lax.all_to_all(outgoing, 'expert', split_axis=0, concat_axis=0, tiled=True)]
    all_to_all x3 -> x0, waiting for transfers between devices: 38.5 us -> none  [the longest x2 33.1 us: from_everyone(): return lax.all_to_all(copies, axis, split_axis=0, concat_axis=0, tiled=True)]
    all_gather x1 -> x0, waiting for transfers between devices: 35.2 us -> none  [gathered_by_axis(): out = lax.all_gather(out, axes[number], axis=dim, tiled=True)]
    unnamed x4 -> x0, waiting for transfers between devices: 19.9 us -> none
    all_to_all x3 -> x0, starting transfers between devices: 18.8 us -> none  [the longest x2 14 us: from_everyone(): return lax.all_to_all(copies, axis, split_axis=0, concat_axis=0, tiled=True)]
    dot_general x5 -> x0, matrix products: 18.4 us -> none  [the longest x1 8.14 us: per_device(): lax.dot_general(down_cols, hidden, (((0,), (1,)), ((), ())), preferred_el...]
  transfers between devices with their start and end apart: 6 -> 0, of which waited for: 6 -> 0; matrix products, arithmetic and copies ran while one was open for 4% -> 0% of each run, Pallas kernels for 0% -> 0%
where the time goes in v2:
time: 96.3 us; the launch traced here: 95.3 us
  Pallas kernels  94 us (98%)
  between operations  1.29 us (1%)
    pallas_call x1, Pallas kernels, per_device(): pl.pallas_call(kernel, out_shape=(jax.ShapeDtypeStruct((TOK, COL), BF), j...  92 us
    pallas_call x1, Pallas kernels, per_device(): pl.pallas_call(pass_on, out_shape=shapes, in_specs=[anywhere] * 2, out_sp...  2.02 us

profile of v2, /device:TPU:2, one launch (start us, length us, event | category | flops | bytes accessed | tf_op | source)
XLA Modules:
  0.0 95.3 jit_solution(5764605817754884175)
XLA Ops:
  1.3 92.0 %shard_map.104 = (bf16[128,128]{1,0:T(8,128)(2,1)}, bf16[4096,128]{1,0:T(8,128)(2,1)}) custom-call(bf16[4,4096]{1,0:T(4,128)(2,1)} %bitcast.17, s32[2,128]{1,0:T(2,128)} %bitcast.19, bf16[8,4096]{1,0:T(8,128)(2,1)} %bitcast.16, bf16[4096,384]{1,0:T(8,128)(2,1)} %bitcast.12, bf16[4096,384]{1,0:T(8,128)(2,1)} %bitcast.13, bf16[384,4096]{1,0:T(8,128)(2,1)} %bitcast.14, ...), custom_call_target="tpu_custom_call" | custom-call | tf_op jit(solution)/shard_map/pallas_call | solution.py:552
  93.2 2.0 %shard_map.105 = (bf16[128,128]{1,0:T(8,128)(2,1)}, bf16[4096,128]{1,0:T(8,128)(2,1)}) custom-call(bf16[128,128]{1,0:T(8,128)(2,1)} %get-tuple-element.6.adapted_h, bf16[4096,128]{1,0:T(8,128)(2,1)} %get-tuple-element.7.clipped_h), custom_call_target="tpu_custom_call" | custom-call | tf_op jit(solution)/shard_map/pallas_call | solution.py:584

commit v3 on v2

--- a/solution.py
+++ b/solution.py
@@ -18,12 +18,14 @@
 FD = 384
 COL = 128
 SLOTS = NE * CAP
-GROUPS = (((0, 240, 1, True), (240, 144, 2, False)),)
-WIDE = ((0, 80, 1, True), (80, 48, 2, True))
+GROUPS = (((0, 240, 1, 1, 0), (240, 144, 2, 0, 1)),)
+WIDE = ((0, 80, 1, 1, 0), (80, 48, 2, 1, 1))
+LAST = ((0, 80, 1, 1, 1), (80, 48, 2, 1, 1))
 PARTS = tuple(part for group in GROUPS for part in group)
-RATE = 46.6e3
-FIRST_HOP, NEXT_HOP, LEAD = 2.2, 0.75, 0.8
+RATE = {("z", True): 50e3, ("z", False): 43e3, ("y", True): 48.5e3, ("y", False): 44.5e3}
+FIRST_HOP, NEXT_HOP, LEAD = 3.0, 0.75, 0.8
 BIAS, U_BIAS = (0.0, 0.0), 0.0
+U_AFTER = ()
 
 
 def dot(a, b, dims=(((1,), (0,)), ((), ()))):
@@ -45,20 +47,22 @@
     return 1 if v % 2 == 0 else -1
 
 
-def spread(kind, skip):
+def spread(kind, zmode, ymode):
     out = []
 
     def along(b, s0):
         for s in (1, -1):
             out.append((0, b, s, 0))
-            if skip:
-                out.append((0, b, 2 * s, 0))
-                out.append((-2 * s, b, s, 0))
+            if zmode == 2:
+                out.extend(((0, b, 2 * s, 0), (0, b, 3 * s, 0)))
+                if s == s0:
+                    out.append((0, b, 4 * s, 0))
+            elif zmode == 1:
+                out.extend(((0, b, 2 * s, 0), (-2 * s, b, s, 0)))
                 if s == s0:
                     out.append((-2 * s, b, 2 * s, 0))
             else:
-                out.append((-s, b, s, 0))
-                out.append((-2 * s, b, s, 0))
+                out.extend(((-s, b, s, 0), (-2 * s, b, s, 0)))
                 if s == s0:
                     out.append((-3 * s, b, s, 0))
 
@@ -66,7 +70,7 @@
         along(0, 1)
         for a in range(-3, 5):
             sg = parity(a)
-            out.extend(((a, 0, 0, 1), (a, 0, 0, -1), (a, -sg, 0, sg)))
+            out.extend(((a, 0, 0, 1), (a, 0, 0, -1), (a, 0, 0, 2 * sg) if ymode else (a, -sg, 0, sg)))
     else:
         out.extend(((0, 0, 0, 1), (0, 0, 0, -1), (0, 0, 0, 2)))
         for b in range(-1, 3):
@@ -86,7 +90,7 @@
         self.bias = 0.0
 
     def send(self, needs, makes, link, size, hops, act, wait, work=0.02):
-        self.nodes.append(dict(needs=needs, makes=makes, link=link, cost=size / RATE, hops=hops, act=act, work=work, bias=self.bias))
+        self.nodes.append(dict(needs=needs, makes=makes, link=link, cost=size / RATE[link], hops=hops, act=act, work=work, bias=self.bias))
         self.waits[makes] = wait
 
     def post(self, needs, makes, delay, act, wait, work=0.1):
@@ -172,12 +176,12 @@
     f = lax.axis_index("ffn")
     z, y = f // NY, f % NY
     core = e % 2
-    turn_z = {1: 1 - 2 * core, 2: 1 - 2 * ((y + core) % 2)}
-    turn_y = {1: 1 - 2 * ((z + core) % 2), 2: 1}
+    turn = 1 - 2 * core
+    turn_y = {1: turn, 2: 1}
     first_dims = (((0,), (0,)), ((), ()))
 
     def spot(kind, da, db):
-        zi = (z + turn_z[kind] * da + 2 * NZ) % NZ
+        zi = (z + turn * da + 2 * NZ) % NZ
         yi = (y + turn_y[kind] * db + 2 * NY) % NY
         return zi * NY + yi
 
@@ -218,6 +222,11 @@
     seven = pl.ds(0, CAP * (NE - 1))
     mine = pl.ds(pl.multiple_of(e * CAP, CAP), CAP)
     next_f, next_e = (f + 1) % NF, (e + 1) % NE
+
+    peers = [(e // 2 + chip) % (NE // 2) * 2 + other for chip in (2, 1, 3) for other in (0, 1)] + [e + turn]
+
+    def theirs(peer):
+        return pl.ds(pl.multiple_of(peer * CAP, CAP), CAP)
 
     def loaded(n):
         plan.waits["load", n] = loads[n].wait
@@ -270,21 +279,19 @@
             xf[TF * n:TF * (n + 1), :] = xr[n].astype(F32)
         xc[...] = dot((ones[0] + ones[1]).astype(BF), xf[...].astype(BF)).astype(BF)
 
-        @pl.loop(1, NE)
-        def _(j):
-            peer = (e + j) % NE
-            theirs = pl.ds(pl.multiple_of(peer * CAP, CAP), CAP)
-            remote(xc.at[theirs], a.at[mine, block(f)], pk_s, pk_r, expert=peer).start()
+        for peer in peers:
+            remote(xc.at[theirs(peer)], a.at[mine, block(f)], pk_s, pk_r, expert=peer).start()
 
         a[mine, block(f)] = xc[mine, :]
 
     packed = remote(xc.at[seven], rc.at[seven], pk_s, pk_r, expert=next_e)
-    plan.post(["columns", "slots"], "packed", 4.3, pack, packed.wait_recv, 0.2)
+    plan.compute(["columns", "slots"], "packing", 0.3, pack)
+    plan.post(["packing"], "packed", 4.3, lambda: None, packed.wait_recv, 0.0)
 
     def gather(name, buf, parts, ssem, rsem, start, chunk_work, on_chunk, extra=(), before=()):
         pieces = {}
-        for p, (row, rows, kind, skip) in enumerate(parts):
-            for da, db, sa, sb in spread(kind, skip):
+        for p, (row, rows, kind, zmode, ymode) in enumerate(parts):
+            for da, db, sa, sb in spread(kind, zmode, ymode):
                 def act(p=p, row=row, rows=rows, kind=kind, da=da, db=db, sa=sa, sb=sb):
                     ref = buf.at[pl.ds(row, rows), block(spot(kind, da, db))]
                     remote(ref, ref, ssem.at[p], rsem.at[p, spot(kind, da, db)], ffn=spot(kind, sa, sb)).start()
@@ -298,7 +305,7 @@
                 held = (name, p, da, db) if (da, db) != (0, 0) else start
                 makes = (name, p, ra, rb)
                 pieces.setdefault(abs(ra), []).append(makes)
-                plan.send([held, *before], makes, towards(sa, sb), rows * COL * 2, abs(sa) + abs(sb), act, wait)
+                plan.send([held, *(before if held != start else ())], makes, towards(sa, sb), rows * COL * 2, abs(sa) + abs(sb), act, wait)
         for k in range(5):
             for s in ((1,) if k in (0, 4) else (1, -1)):
                 needs = [start, *pieces[k], *extra]
@@ -309,12 +316,12 @@
         return [(name, "chunk", k, s) for k in range(5) for s in ((1,) if k in (0, 4) else (1, -1))]
 
     def gather_done(buf, parts, ssem):
-        for p, (row, rows, _, _) in enumerate(parts):
+        for p, (row, rows, *_) in enumerate(parts):
             ref = buf.at[pl.ds(row, rows), pl.ds(0, COL * (NF - 1))]
             remote(ref, ref, ssem.at[p], lg_r.at[0, 0], ffn=next_f).wait_send()
 
     plan.bias = U_BIAS
-    ups_all = gather("u", ups, WIDE, ug_s, ug_r, loaded(3), 0.0, lambda zi, first: None)
+    ups_all = gather("u", ups, WIDE, ug_s, ug_r, loaded(3), 0.0, lambda zi, first: None, (), U_AFTER)
 
     fins = []
     for g, group in enumerate(GROUPS):
@@ -351,7 +358,7 @@
 
             plan.compute([("hid", g), loaded(6)], ("pb", g, k), (0.3 if k in (0, 4) else 0.6) * size / SLOTS, down)
 
-        for p, (row, rows, kind, skip) in enumerate(group):
+        for p, (row, rows, kind, *_) in enumerate(group):
             buf, q = bufs[2 * g + p], 2 * g + p
             slots = {}
 
@@ -433,11 +440,8 @@
     plan.bias = 0.0
 
     def give_back():
-        @pl.loop(1, NE)
-        def _(j):
-            peer = (e + j) % NE
-            theirs = pl.ds(pl.multiple_of(peer * CAP, CAP), CAP)
-            remote(fin.at[theirs], rc.at[mine], rt_s, rt_r, expert=peer).start()
+        for peer in peers:
+            remote(fin.at[theirs(peer)], rc.at[mine], rt_s, rt_r, expert=peer).start()
 
         rc[mine, :] = fin[mine, :]
 
@@ -507,7 +511,7 @@
             acc[...] += term
 
     plan.compute(["layer"], ("early", 0), 0.01, lambda: None)
-    gather("l", lay, WIDE, lg_s, lg_r, "layer", 0.16, adapter_chunk, ("factor", loaded(7)))
+    gather("l", lay, LAST, lg_s, lg_r, "layer", 0.16, adapter_chunk, ("factor", loaded(7)))
     plan.emit()
 
     oa[...] = (lay[:, block(f)].astype(F32) + acc[...]).astype(BF)
@@ -519,9 +523,9 @@
     returned.wait_send()
     norms.wait_send()
     gather_done(ups, WIDE, ug_s)
-    gather_done(lay, WIDE, lg_s)
+    gather_done(lay, LAST, lg_s)
     gather_done(a, PARTS, ag_s)
-    for q, (_, rows, _, _) in enumerate(PARTS):
+    for q, (_, rows, *_) in enumerate(PARTS):
         ref = bufs[q].at[pl.ds(0, NF - 1)]
         remote(ref, ref, rs_s.at[q], rs_r.at[q, 0], ffn=next_f).wait_send()
     first_out.wait()

time: 96.3 us -> 92.3 us (0.958)
  Pallas kernels: 94 us -> 90.9 us
    pallas_call x1, Pallas kernels: 92 us -> 88.9 us  [per_device(): pl.pallas_call(kernel, out_shape=(jax.ShapeDtypeStruct((TOK, COL), BF), j...]
where the time goes in v3:
time: 92.3 us; the launch traced here: 92.2 us
  Pallas kernels  90.9 us (98%)
  between operations  1.29 us (1%)
    pallas_call x1, Pallas kernels, per_device(): pl.pallas_call(kernel, out_shape=(jax.ShapeDtypeStruct((TOK, COL), BF), j...  88.9 us
    pallas_call x1, Pallas kernels, per_device(): pl.pallas_call(pass_on, out_shape=shapes, in_specs=[anywhere] * 2, out_sp...  2.02 us

profile of v3, /device:TPU:2, one launch (start us, length us, event | category | flops | bytes accessed | tf_op | source)
XLA Modules:
  0.0 92.2 jit_solution(1243064977434741779)
XLA Ops:
  1.3 88.9 %shard_map.104 = (bf16[128,128]{1,0:T(8,128)(2,1)}, bf16[4096,128]{1,0:T(8,128)(2,1)}) custom-call(bf16[4,4096]{1,0:T(4,128)(2,1)} %bitcast.17, s32[2,128]{1,0:T(2,128)} %bitcast.19, bf16[8,4096]{1,0:T(8,128)(2,1)} %bitcast.16, bf16[4096,384]{1,0:T(8,128)(2,1)} %bitcast.12, bf16[4096,384]{1,0:T(8,128)(2,1)} %bitcast.13, bf16[384,4096]{1,0:T(8,128)(2,1)} %bitcast.14, ...), custom_call_target="tpu_custom_call" | custom-call | tf_op jit(solution)/shard_map/pallas_call | solution.py:556
  90.1 2.0 %shard_map.105 = (bf16[128,128]{1,0:T(8,128)(2,1)}, bf16[4096,128]{1,0:T(8,128)(2,1)}) custom-call(bf16[128,128]{1,0:T(8,128)(2,1)} %get-tuple-element.6.adapted_h, bf16[4096,128]{1,0:T(8,128)(2,1)} %get-tuple-element.7.clipped_h), custom_call_target="tpu_custom_call" | custom-call | tf_op jit(solution)/shard_map/pallas_call | solution.py:588

commit v4 on v3

--- a/solution.py
+++ b/solution.py
@@ -18,9 +18,9 @@
 FD = 384
 COL = 128
 SLOTS = NE * CAP
-GROUPS = (((0, 240, 1, 1, 0), (240, 144, 2, 0, 1)),)
-WIDE = ((0, 80, 1, 1, 0), (80, 48, 2, 1, 1))
-LAST = ((0, 80, 1, 1, 1), (80, 48, 2, 1, 1))
+GROUPS = (((0, 240, 1, 1, 4), (240, 144, 2, 0, 0)),)
+WIDE = ((0, 80, 1, 1, 5), (80, 48, 2, 1, 0))
+LAST = ((0, 80, 1, 1, 1), (80, 48, 2, 1, 0))
 PARTS = tuple(part for group in GROUPS for part in group)
 RATE = {("z", True): 50e3, ("z", False): 43e3, ("y", True): 48.5e3, ("y", False): 44.5e3}
 FIRST_HOP, NEXT_HOP, LEAD = 3.0, 0.75, 0.8
@@ -70,7 +70,7 @@
         along(0, 1)
         for a in range(-3, 5):
             sg = parity(a)
-            out.extend(((a, 0, 0, 1), (a, 0, 0, -1), (a, 0, 0, 2 * sg) if ymode else (a, -sg, 0, sg)))
+            out.extend(((a, 0, 0, 1), (a, 0, 0, -1), (a, 0, 0, 2 * sg) if abs(a) >= ymode else (a, -sg, 0, sg)))
     else:
         out.extend(((0, 0, 0, 1), (0, 0, 0, -1), (0, 0, 0, 2)))
         for b in range(-1, 3):

time: 92.3 us -> 92 us (level)
  no operation moved by 1% of the time
where the time goes in v4:
time: 92 us; the launch traced here: 91.7 us
  Pallas kernels  90.4 us (98%)
  between operations  1.29 us (1%)
    pallas_call x1, Pallas kernels, per_device(): pl.pallas_call(kernel, out_shape=(jax.ShapeDtypeStruct((TOK, COL), BF), j...  88.4 us
    pallas_call x1, Pallas kernels, per_device(): pl.pallas_call(pass_on, out_shape=shapes, in_specs=[anywhere] * 2, out_sp...  2.02 us

profile of v4, /device:TPU:2, one launch (start us, length us, event | category | flops | bytes accessed | tf_op | source)
XLA Modules:
  0.0 91.7 jit_solution(6708737601994863064)
XLA Ops:
  1.3 88.4 %shard_map.104 = (bf16[128,128]{1,0:T(8,128)(2,1)}, bf16[4096,128]{1,0:T(8,128)(2,1)}) custom-call(bf16[4,4096]{1,0:T(4,128)(2,1)} %bitcast.17, s32[2,128]{1,0:T(2,128)} %bitcast.19, bf16[8,4096]{1,0:T(8,128)(2,1)} %bitcast.16, bf16[4096,384]{1,0:T(8,128)(2,1)} %bitcast.12, bf16[4096,384]{1,0:T(8,128)(2,1)} %bitcast.13, bf16[384,4096]{1,0:T(8,128)(2,1)} %bitcast.14, ...), custom_call_target="tpu_custom_call" | custom-call | tf_op jit(solution)/shard_map/pallas_call | solution.py:556
  89.7 2.0 %shard_map.105 = (bf16[128,128]{1,0:T(8,128)(2,1)}, bf16[4096,128]{1,0:T(8,128)(2,1)}) custom-call(bf16[128,128]{1,0:T(8,128)(2,1)} %get-tuple-element.6.adapted_h, bf16[4096,128]{1,0:T(8,128)(2,1)} %get-tuple-element.7.clipped_h), custom_call_target="tpu_custom_call" | custom-call | tf_op jit(solution)/shard_map/pallas_call | solution.py:588
